TPU v7x, 32 devices: a whole 2x2x4 slice. The times are simulated.
32 devices in a mesh: dp: 8 (over z, x), mp: 4 (over y, core).
Axes of the slice: x: 2, y: 2, z: 4, core: 2. Of those that a mesh axis runs over, the one named last changes fastest.
Arguments:
- hidden: bfloat16 [2048, 8192], P('dp', 'mp'), may hold values from -6 to 6
- norm_gain: bfloat16 [8192], P('mp'), may hold values from 0.5 to 1.5
- kv_weight: bfloat16 [8192, 2048], P(None, 'mp'), may hold values from -0.0625 to 0.0625
- clip_upper: float32 [64, 2048], P(None, 'mp'), may hold values from 0.5 to 4
- clip_lower: float32 [64, 2048], P(None, 'mp'), may hold values from 0.5 to 4
Outputs:
- upper_final: float32 [64, 2048], P('dp', 'mp')
- lower_final: float32 [64, 2048], P('dp', 'mp')
All inputs are finite; a program needn't handle non-finite values.
Results may differ from a plain program's by a relative error of at most 0.012.
Values may be sent and summed in bfloat16 or wider, within the bound.
A program may use at most 64 MiB of HBM per device.

v0:
```python
import math

import jax
import jax.numpy as jnp
from jax import lax
from jax.sharding import PartitionSpec as P

D = 8192
KVW = 1024
GROUP = 128
STEPS = 2


norm_eps = 1e-05
grad_eps = 1e-06
learn_rate = 0.25
top_level = 15.0
two_pi = 2.0 * math.pi


def fake_quant(upper, lower, grouped, magnitude):
    top_clip = jax.nn.sigmoid(upper) * magnitude
    bottom_clip = jax.nn.sigmoid(lower) * magnitude
    quant_step = (top_clip + bottom_clip + 1e-06) / top_level
    zero_point = bottom_clip / quant_step
    level = jnp.clip(grouped / quant_step[:, None, :] + zero_point[:, None, :], 0.0, top_level)
    soft_level = level - jnp.sin(two_pi * level) / two_pi
    fake = (soft_level - zero_point[:, None, :]) * quant_step[:, None, :]
    return fake.reshape(grouped.shape[0] * grouped.shape[1], grouped.shape[2])


def clip_gradients(upper, lower, grouped, magnitude, normed, targets):

    def quantizer(first, second):
        return fake_quant(first, second, grouped, magnitude)

    fake, pullback = jax.vjp(quantizer, upper, lower)
    quantized = fake.astype(jnp.bfloat16)
    output = jnp.dot(normed, quantized, preferred_element_type=jnp.float32)
    misfit = (output - targets).astype(jnp.bfloat16)
    cotangent = lax.dot_general(
        normed, misfit, (((0,), (0,)), ((), ())), preferred_element_type=jnp.float32
    )
    return pullback(cotangent)


def body(hidden, norm_gain, kv_weight, clip_upper, clip_lower):
    columns = kv_weight.shape[1]
    grouped = kv_weight.astype(jnp.float32).reshape(D // GROUP, GROUP, columns)
    magnitude = jnp.max(jnp.abs(grouped), axis=1)
    gathered, gathered_gain = (
        lax.all_gather(hidden, "mp", axis=1, tiled=True),
        lax.all_gather(norm_gain[None, :], "mp", axis=1, tiled=True),
    )
    hidden_f = gathered.astype(jnp.float32)
    mean_sq = jnp.mean(hidden_f * hidden_f, axis=1, keepdims=True)
    normed = (
        hidden_f * lax.rsqrt(mean_sq + norm_eps) * gathered_gain[0].astype(jnp.float32)
    ).astype(jnp.bfloat16)
    targets = jnp.dot(normed, kv_weight, preferred_element_type=jnp.float32)
    param_count = 4 * (D // GROUP) * KVW
    share_rows = D // GROUP // lax.axis_size("dp")
    first_row = lax.axis_index("dp") * share_rows
    upper, lower = (clip_upper, clip_lower)
    for iteration in range(STEPS):
        grad_up, grad_low = clip_gradients(upper, lower, grouped, magnitude, normed, targets)
        grad_up, grad_low = lax.psum((grad_up, grad_low), "dp")
        local_sq = jnp.sum(grad_up * grad_up) + jnp.sum(grad_low * grad_low)
        total_sq = lax.psum(local_sq, "mp")
        grad_rms = jnp.sqrt(total_sq / param_count + grad_eps)
        upper = upper - learn_rate * grad_up / grad_rms
        lower = lower - learn_rate * grad_low / grad_rms
    upper = lax.dynamic_slice_in_dim(upper, first_row, share_rows, 0)
    lower = lax.dynamic_slice_in_dim(lower, first_row, share_rows, 0)
    return (upper, lower)


def solution(mesh):
    in_specs = (P("dp", "mp"), P("mp"), P(None, "mp"), P(None, "mp"), P(None, "mp"))
    out_specs = (P("dp", "mp"), P("dp", "mp"))
    return jax.shard_map(body, mesh=mesh, in_specs=in_specs, out_specs=out_specs, check_vma=False)
```

profile of v0, /device:TPU:0, one launch (start us, length us, event | category | flops | bytes accessed | tf_op | source)
XLA Modules:
  0.0 513.9 jit_solution(16978895213195059131)
XLA Ops:
  7.2 0.0 all-gather.3.cloned.1.call-start
  7.2 0.7 all-gather.3.cloned.1.call-update
  7.9 0.0 all-reduce.7.cloned.1.call-start
  8.0 6.5 %all-gather = bf16[8192]{0:T(1024)(128)(2,1)S(1)} all-gather(bf16[2048]{0:T(1024)(128)(2,1)} %param.9), channel_id=2, replica_groups=mesh['dp'=8,'mp'=4] {'mp'}, dimensions={0}, use_global_device_ids=true | all-gather | bytes 20480 | tf_op jit(solution)/shard_map/all_gather | solution.py:53
  14.5 6.2 %fusion = f32[64,512]{1,0:T(8,128)S(1)} fusion(bf16[8192,512]{1,0:T(8,128)(2,1)} %param.10), kind=kLoop, calls=%fused_computation.5 | loop fusion | flops 12550144 | bytes 8519680 | tf_op jit(solution)/shard_map/reduce_max | solution.py:50
  20.7 0.1 multiply_divide_fusion.1
  20.8 0.1 fusion.25
  20.9 60.6 %multiply_convert_fusion.1 = bf16[64,128,512]{2,1,0:T(8,128)(2,1)} fusion(f32[64,512]{1,0:T(8,128)S(1)} %get-tuple-element.31, f32[64,512]{1,0:T(8,128)S(1)} %fusion.25, bf16[8192,512]{1,0:T(8,128)(2,1)S(1)} %copy-done), kind=kLoop, calls=%fused_computation.18 | loop fusion | flops 41943040 | bytes 17039360 | tf_op jit(solution)/shard_map/convert_element_type | solution.py:38
  81.5 3.3 fusion.7
  84.8 7.4 %fusion.28 = f32[256,512]{1,0:T(8,128)S(1)} fusion(bf16[8192,512]{1,0:T(8,128)(2,1)} %param.10, bf16[256,8192]{1,0:T(8,128)(2,1)} %all-gather.3.cloned.1.call-done, f32[8192]{0:T(1024)S(1)} %mul.266, f32[256]{0:T(256)S(1)} %add_rsqrt_fusion), kind=kOutput, calls=%fused_computation.76 | convolution fusion | flops 2155872256 | bytes 13140992 | tf_op jit(solution)/shard_map/dot_general | solution.py:60
  92.3 0.3 slice-done.5
  92.5 2.4 fusion.12.clone.1.clone.2
  94.9 94.1 %fusion.11 = (f32[64,512]{1,0:T(8,128)S(1)}, f32[64,512]{1,0:T(8,128)S(1)}, f32[64,512]{1,0:T(8,128)S(1)}, f32[64,512]{1,0:T(8,128)S(1)}) fusion(f32[64,512]{1,0:T(8,128)S(1)} %fusion.25, bf16[8192,512]{1,0:T(8,128)(2,1)S(1)} %bitcast.58, f32[64,512]{1,0:T(8,128)S(1)} %get-tuple-element.31, f32[64,512]{1,0:T(8,128)S(1)} %get-tuple-element.30, ...), kind=kOutput, calls=%fused_computation.30 | convolution fusion | flops 2289958912 | bytes 13796352 | tf_op jit(solution)/shard_map/dot_general | solution.py:41
  189.0 0.9 fusion.17
  189.9 0.0 all-reduce.7.cloned.1.call-update
  189.9 0.0 all-reduce.5.cloned.1.call-start
  190.0 73.2 %all-reduce.7.cloned.1.call-done = (f32[64,512]{1,0:T(8,128)}, f32[64,512]{1,0:T(8,128)}) async-done(((f32[64,512]{1,0:T(8,128)}, f32[64,512]{1,0:T(8,128)}), (f32[64,512]{1,0:T(8,128)}, f32[64,512]{1,0:T(8,128)})) %all-reduce.7.cloned.1.call-update) | async-done | bytes 262160 | tf_op jit(solution)/shard_map/psum | solution.py:67
  263.2 1.6 multiply_reduce_fusion.6
  266.1 6.2 %psum.44 = f32[]{:T(128)} all-reduce(f32[]{:T(128)S(6)} %add.87), channel_id=1, replica_groups=mesh['dp'=8,'mp'=4] {'mp'}, use_global_device_ids=true, to_apply=%region_10.12 | all-reduce | flops 1 | bytes 8 | tf_op jit(solution)/shard_map/psum | solution.py:69
  272.9 1.1 multiply_divide_fusion
  274.0 0.1 fusion.24
  274.1 60.9 %multiply_convert_fusion = bf16[64,128,512]{2,1,0:T(8,128)(2,1)S(1)} fusion(f32[64,512]{1,0:T(8,128)S(1)} %get-tuple-element.27, f32[64,512]{1,0:T(8,128)S(1)} %fusion.24, bf16[8192,512]{1,0:T(8,128)(2,1)} %param.10), kind=kLoop, calls=%fused_computation.15 | loop fusion | flops 41943040 | bytes 17039360 | tf_op jit(solution)/shard_map/convert_element_type | solution.py:38
  335.0 2.4 fusion.14.clone.1.clone.5
  337.5 83.8 %fusion.10 = (f32[64,512]{1,0:T(8,128)S(1)}, f32[64,512]{1,0:T(8,128)S(1)}, f32[64,512]{1,0:T(8,128)S(1)}, f32[64,512]{1,0:T(8,128)S(1)}) fusion(f32[64,512]{1,0:T(8,128)S(1)} %fusion.24, bf16[8192,512]{1,0:T(8,128)(2,1)S(1)} %bitcast.60, f32[64,512]{1,0:T(8,128)S(1)} %get-tuple-element.27, f32[64,512]{1,0:T(8,128)S(1)} %get-tuple-element.26, ...), kind=kOutput, calls=%fused_computation.29 | convolution fusion | flops 2289958912 | bytes 13796352 | tf_op jit(solution)/shard_map/dot_general | solution.py:41
  421.2 0.9 fusion.19
  422.1 0.0 all-reduce.5.cloned.1.call-update
  422.1 71.0 %all-reduce.5.cloned.1.call-done = (f32[64,512]{1,0:T(8,128)}, f32[64,512]{1,0:T(8,128)}) async-done(((f32[64,512]{1,0:T(8,128)}, f32[64,512]{1,0:T(8,128)}), (f32[64,512]{1,0:T(8,128)}, f32[64,512]{1,0:T(8,128)})) %all-reduce.5.cloned.1.call-update) | async-done | bytes 262160 | tf_op jit(solution)/shard_map/psum | solution.py:67
  493.1 1.5 multiply_reduce_fusion.4
  494.6 1.5 multiply_reduce_fusion.5
  497.5 6.2 %psum.47 = f32[]{:T(128)} all-reduce(f32[]{:T(128)S(6)} %add.95), channel_id=1, replica_groups=mesh['dp'=8,'mp'=4] {'mp'}, use_global_device_ids=true, to_apply=%region_19.21 | all-reduce | flops 1 | bytes 8 | tf_op jit(solution)/shard_map/psum | solution.py:69
  504.3 1.3 dynamic-slice_subtract_fusion
  505.7 1.3 dynamic-slice_subtract_fusion.1
  (27 shorter events, 0.1 us)
Async XLA Ops:
  7.2 13.5 %copy-start.4 = (f32[64,512]{1,0:T(8,128)S(1)}, f32[64,512]{1,0:T(8,128)}, u32[]{:S(2)}) copy-start(f32[64,512]{1,0:T(8,128)} %param.11) | copy-start | bytes 393220
  7.2 13.5 %copy-start.3 = (f32[64,512]{1,0:T(8,128)S(1)}, f32[64,512]{1,0:T(8,128)}, u32[]{:S(2)}) copy-start(f32[64,512]{1,0:T(8,128)} %param.12) | copy-start | bytes 393220
  7.2 74.3 %all-gather.3.cloned.1.call-start = ((), (), s32[]{:S(2)}) async-start(), calls=%async_computation | async-start | bytes 5242880 | tf_op jit(solution)/shard_map/all_gather | solution.py:52
  7.9 255.2 %all-reduce.7.cloned.1.call-start = ((), (), s32[]{:S(2)}) async-start(), calls=%async_computation.2 | async-start | bytes 524288 | tf_op jit(solution)/shard_map/psum | solution.py:67
  8.0 12.9 %copy-start = (bf16[8192,512]{1,0:T(8,128)(2,1)S(1)}, bf16[8192,512]{1,0:T(8,128)(2,1)}, u32[]{:S(2)}) copy-start(bf16[8192,512]{1,0:T(8,128)(2,1)} %param.10) | copy-start | bytes 25165828
  81.5 10.7 %slice-start.4 = ((s8[8388608]{0:T(1024)(128)(4,1)}), s8[4194304]{0:T(1024)(128)(4,1)S(1)}, s32[]{:S(2)}) async-start(s8[8388608]{0:T(1024)(128)(4,1)} %bitcast.61), calls=%async_computation.7 | async-start | bytes 8388608
  81.5 13.4 %slice-start = ((s8[8388608]{0:T(1024)(128)(4,1)}), s8[4194304]{0:T(1024)(128)(4,1)S(1)}, s32[]{:S(2)}) async-start(s8[8388608]{0:T(1024)(128)(4,1)} %bitcast.57), calls=%async_computation.3 | async-start | bytes 8388608
  84.8 7.8 %slice-start.5 = ((s8[8388608]{0:T(1024)(128)(4,1)}), s8[4194304]{0:T(1024)(128)(4,1)S(1)}, s32[]{:S(2)}) async-start(s8[8388608]{0:T(1024)(128)(4,1)} %bitcast.61), calls=%async_computation.8 | async-start | bytes 8388608
  84.8 7.8 %copy-start.1 = (bf16[256,8192]{1,0:T(8,128)(2,1)S(1)}, bf16[256,8192]{1,0:T(8,128)(2,1)}, u32[]{:S(2)}) copy-start(bf16[256,8192]{1,0:T(8,128)(2,1)} %all-gather.3.cloned.1.call-done) | copy-start | bytes 12582916
  84.8 10.1 %slice-start.1 = ((s8[8388608]{0:T(1024)(128)(4,1)}), s8[4194304]{0:T(1024)(128)(4,1)S(1)}, s32[]{:S(2)}) async-start(s8[8388608]{0:T(1024)(128)(4,1)} %bitcast.57), calls=%async_computation.4 | async-start | bytes 8388608
  189.9 303.2 %all-reduce.5.cloned.1.call-start = ((), (), s32[]{:S(2)}) async-start(), calls=%async_computation.1 | async-start | bytes 524288 | tf_op jit(solution)/shard_map/psum | solution.py:67
  274.1 60.9 %copy-start.2 = (bf16[256,8192]{1,0:T(8,128)(2,1)S(1)}, bf16[256,8192]{1,0:T(8,128)(2,1)}, u32[]{:S(2)}) copy-start(bf16[256,8192]{1,0:T(8,128)(2,1)} %all-gather.3.cloned.1.call-done) | copy-start | bytes 12582916
  274.1 63.3 %slice-start.2 = ((s8[8388608]{0:T(1024)(128)(4,1)}), s8[4194304]{0:T(1024)(128)(4,1)S(1)}, s32[]{:S(2)}) async-start(s8[8388608]{0:T(1024)(128)(4,1)} %bitcast.59), calls=%async_computation.5 | async-start | bytes 8388608
  335.0 2.4 slice-start.3
Sparse Core Ops, SparseCore 0:
  9.6 37.1 all-gather.2
  190.0 73.0 all-reduce.6
  422.2 70.8 all-reduce.4
where the time goes:
time: 521 us; the launch traced here: 514 us
  matrix products  190 us (36%)
  waiting for transfers between devices  145 us (28%)
  other arithmetic  141 us (27%)
  blocking collectives  18.9 us (4%)
  between operations  18.4 us (4%)
    dot_general x2, matrix products, clip_gradients(): lax.dot_general(normed, misfit, (((0,), (0,)), ((), ())), preferred_eleme...  178 us
    psum x2, waiting for transfers between devices, body(): grad_up, grad_low = lax.psum((grad_up, grad_low), 'dp')  144 us
    convert_element_type x2, other arithmetic, clip_gradients(): quantized = fake.astype(jnp.bfloat16)  121 us
    psum x2, blocking collectives, body(): total_sq = lax.psum(local_sq, 'mp')  12.3 us
  transfers between devices with their start and end apart: 3, of which 2 were waited for; matrix products, arithmetic and copies ran while one was open for 13% of the time, Pallas kernels for 0%

commit v1 on v0

v1 whole, which is shorter than its diff:
```python
import functools
import math

import jax
import jax.numpy as jnp
from jax import lax
from jax.experimental import pallas as pl
from jax.experimental.pallas import tpu as pltpu
from jax.sharding import PartitionSpec as P

GROUP = 128
STEPS = 2
CHUNK = 8
LANES = 128

norm_eps = 1e-05
grad_eps = 1e-06
learn_rate = 0.25
top_level = 15.0

bf16, f32 = jnp.bfloat16, jnp.float32
ROUNDER = 12582912.0
SIN = (3.99733775, -10.17843475, 8.93899279)
COS = (0.99996212, -3.73207042, 4.98340402, -2.88721551)


def clip_params(upper, lower, magnitude):
    sig_up, sig_low = jax.nn.sigmoid(upper), jax.nn.sigmoid(lower)
    top, bottom = sig_up * magnitude, sig_low * magnitude
    step = (top + bottom + 1e-06) / top_level
    return sig_up, sig_low, top, bottom, step


def horner(x, coefs):
    acc = jnp.full_like(x, coefs[-1])
    for c in coefs[-2::-1]:
        acc = acc * x + jnp.asarray(c, x.dtype)
    return acc


def quantize_tile(w, low, high, inverse, zero, step):
    clipped = jnp.minimum(jnp.maximum(w.astype(f32), low), high)
    level = clipped * inverse + zero
    frac = (level - ((level + ROUNDER) - ROUNDER)).astype(bf16)
    x = frac * frac
    sine = frac * (jnp.asarray(0.25, bf16) - x) * horner(x, SIN)
    cosine = (jnp.asarray(1.0, bf16) - jnp.asarray(16.0, bf16) * x) * horner(x, COS)
    quantized = clipped.astype(bf16) - sine * step.astype(bf16)
    return quantized - w, quantized - (w - w * cosine), -cosine


def forward_kernel(w_ref, up_ref, low_ref, diff_ref, h1_ref, h2_ref, mag_ref, par_ref):
    chunk, columns = up_ref.shape
    for g in range(chunk):
        w = w_ref[g * GROUP : (g + 1) * GROUP, :]
        mag_ref[g : g + 1, :] = jnp.max(jnp.abs(w), axis=0, keepdims=True).astype(f32)
    _, _, top, bottom, step = clip_params(up_ref[...], low_ref[...], mag_ref[...])
    inverse = 1.0 / step
    par_ref[0] = -bottom
    par_ref[1] = top + 1e-06
    par_ref[2] = inverse
    par_ref[3] = bottom * inverse
    par_ref[4] = step

    for g in range(chunk):
        rows = pl.ds(g * GROUP, GROUP)
        for c in range(columns // LANES):
            lanes = pl.ds(c * LANES, LANES)
            par = [par_ref[k, g : g + 1, lanes] for k in range(5)]
            diff, h1, h2 = quantize_tile(w_ref[rows, lanes], *par)
            diff_ref[rows, lanes] = diff
            h1_ref[rows, lanes] = h1
            h2_ref[rows, lanes] = h2


def forward(weight, upper, lower):
    rows, columns = weight.shape
    groups = rows // GROUP
    big = pl.BlockSpec((CHUNK * GROUP, columns), lambda i: (i, 0))
    small = pl.BlockSpec((CHUNK, columns), lambda i: (i, 0))
    out = jax.ShapeDtypeStruct((rows, columns), bf16)
    return pl.pallas_call(
        forward_kernel,
        grid=(groups // CHUNK,),
        in_specs=[big, small, small],
        out_specs=[big, big, big, small],
        out_shape=[out, out, out, jax.ShapeDtypeStruct((groups, columns), f32)],
        scratch_shapes=[pltpu.VMEM((5, CHUNK, columns), f32)],
        cost_estimate=pl.CostEstimate(
            flops=30 * rows * columns, bytes_accessed=8 * rows * columns, transcendentals=0
        ),
    )(weight, upper, lower)


def backward_kernel(nt_ref, misfit_ref, h1_ref, h2_ref, up_ref, low_ref, mag_ref, grad_ref, sum_ref):
    chunk, columns = up_ref.shape
    for g in range(chunk):
        rows = pl.ds(g * GROUP, GROUP)
        cot = jnp.dot(nt_ref[rows, :], misfit_ref[...], preferred_element_type=f32)
        sum_ref[0, g : g + 1, :] = jnp.sum(cot * h1_ref[rows, :].astype(f32), axis=0, keepdims=True)
        sum_ref[1, g : g + 1, :] = jnp.sum(cot * h2_ref[rows, :].astype(f32), axis=0, keepdims=True)
    magnitude = mag_ref[...]
    sig_up, sig_low, top, bottom, step = clip_params(up_ref[...], low_ref[...], magnitude)
    t2 = sum_ref[1]
    grad_step = (sum_ref[0] - t2 * bottom) / step
    grad_top = grad_step / top_level
    grad_ref[0] = grad_top * magnitude * sig_up * (1.0 - sig_up)
    grad_ref[1] = (grad_top + t2) * magnitude * sig_low * (1.0 - sig_low)


def backward(normed_t, misfit, h1, h2, upper, lower, magnitude):
    rows, columns = h1.shape
    tokens = misfit.shape[0]
    groups = rows // GROUP
    big = pl.BlockSpec((CHUNK * GROUP, columns), lambda i: (i, 0))
    small = pl.BlockSpec((CHUNK, columns), lambda i: (i, 0))
    return pl.pallas_call(
        backward_kernel,
        grid=(groups // CHUNK,),
        in_specs=[
            pl.BlockSpec((CHUNK * GROUP, tokens), lambda i: (i, 0)),
            pl.BlockSpec((tokens, columns), lambda i: (0, 0)),
            big, big, small, small, small,
        ],
        out_specs=pl.BlockSpec((2, CHUNK, columns), lambda i: (0, i, 0)),
        out_shape=jax.ShapeDtypeStruct((2, groups, columns), f32),
        scratch_shapes=[pltpu.VMEM((2, CHUNK, columns), f32)],
        cost_estimate=pl.CostEstimate(
            flops=2 * tokens * rows * columns, bytes_accessed=5 * rows * columns, transcendentals=0
        ),
    )(normed_t, misfit, h1, h2, upper, lower, magnitude)


def body(hidden, norm_gain, kv_weight, clip_upper, clip_lower):
    gathered = lax.all_gather(hidden, "mp", axis=1, tiled=True)
    gathered_gain = lax.all_gather(norm_gain[None, :], "mp", axis=1, tiled=True)
    hidden_f = gathered.astype(f32)
    mean_sq = jnp.mean(hidden_f * hidden_f, axis=1, keepdims=True)
    normed = (hidden_f * lax.rsqrt(mean_sq + norm_eps) * gathered_gain[0].astype(f32)).astype(bf16)
    normed_t = normed.T
    groups = clip_upper.shape[0]
    param_count = 2 * groups * clip_upper.shape[1] * lax.axis_size("mp")
    share_rows = groups // lax.axis_size("dp")
    first_row = lax.axis_index("dp") * share_rows
    params = jnp.stack([clip_upper, clip_lower])
    for iteration in range(STEPS):
        diff, h1, h2, magnitude = forward(kv_weight, params[0], params[1])
        misfit = jnp.dot(normed, diff, preferred_element_type=f32).astype(bf16)
        grads = backward(normed_t, misfit, h1, h2, params[0], params[1], magnitude)
        if iteration + 1 < STEPS:
            grads = lax.psum(grads, "dp")
            total_sq = lax.psum(jnp.sum(grads * grads), "mp")
        else:
            grads = lax.psum_scatter(grads, "dp", scatter_dimension=1, tiled=True)
            total_sq = lax.psum(jnp.sum(grads * grads), ("dp", "mp"))
            params = lax.dynamic_slice_in_dim(params, first_row, share_rows, 1)
        grad_rms = jnp.sqrt(total_sq / param_count + grad_eps)
        params = params - learn_rate * grads / grad_rms
    return (params[0], params[1])


def solution(mesh):
    in_specs = (P("dp", "mp"), P("mp"), P(None, "mp"), P(None, "mp"), P(None, "mp"))
    out_specs = (P("dp", "mp"), P("dp", "mp"))
    return jax.shard_map(body, mesh=mesh, in_specs=in_specs, out_specs=out_specs, check_vma=False)
```

time: 521 us -> 311 us (0.60); the launches traced: 514 us -> 310 us
  matrix products: 190 us -> 15.2 us
  other arithmetic: 141 us -> 13.1 us
  Pallas kernels: 0 us -> 66.2 us
  blocking collectives: 18.9 us -> 53.2 us
    dot_general x5 -> x2, matrix products: 190 us -> 15.2 us  [body(): misfit = jnp.dot(normed, diff, preferred_element_type=f32).astype(bf16)]
    convert_element_type x2 -> x0, other arithmetic: 121 us -> none  [clip_gradients(): quantized = fake.astype(jnp.bfloat16)]
    psum x2 -> x1, waiting for transfers between devices: 144 us -> 71.1 us  [body(): grads = lax.psum(grads, 'dp')]
    pallas_call x0 -> x4, Pallas kernels: none -> 66.2 us  [the longest x2 41.2 us: forward(): pl.pallas_call(forward_kernel, grid=(groups // CHUNK,), in_specs=[big, sm...]
    reduce_scatter x0 -> x1, waiting for transfers between devices: none -> 62.3 us  [body(): grads = lax.psum_scatter(grads, 'dp', scatter_dimension=1, tiled=True)]
    psum x2, blocking collectives: 12.3 us -> 46.8 us  [the longest x1 40.3 us: body(): total_sq = lax.psum(jnp.sum(grads * grads), ('dp', 'mp'))]
    all_gather x1, waiting for transfers between devices: 0.01 us -> 10.3 us  [body(): gathered = lax.all_gather(hidden, 'mp', axis=1, tiled=True)]
    reduce_max x1 -> x0, other arithmetic: 6.16 us -> none  [body(): magnitude = jnp.max(jnp.abs(grouped), axis=1)]
  transfers between devices with their start and end apart: 3 -> 3, of which waited for: 2 -> 3; matrix products, arithmetic and copies ran while one was open for 13% -> 0% of each run, Pallas kernels for 0% -> 7%
where the time goes in v1:
time: 311 us; the launch traced here: 310 us
  waiting for transfers between devices  144 us (46%)
  Pallas kernels  66.2 us (21%)
  blocking collectives  53.2 us (17%)
  matrix products  15.2 us (5%)
  between operations  15.2 us (5%)
  other arithmetic  13.1 us (4%)
  local copies, waits for them, and re-layouts  3.66 us (1%)
    psum x1, waiting for transfers between devices, body(): grads = lax.psum(grads, 'dp')  71.1 us
    reduce_scatter x1, waiting for transfers between devices, body(): grads = lax.psum_scatter(grads, 'dp', scatter_dimension=1, tiled=True)  62.3 us
    pallas_call x2, Pallas kernels, forward(): pl.pallas_call(forward_kernel, grid=(groups // CHUNK,), in_specs=[big, sm...  41.2 us
    psum x1, blocking collectives, body(): total_sq = lax.psum(jnp.sum(grads * grads), ('dp', 'mp'))  40.3 us
    pallas_call x2, Pallas kernels, backward(): pl.pallas_call(backward_kernel, grid=(groups // CHUNK,), in_specs=[pl.Blo...  25 us
    dot_general x2, matrix products, body(): misfit = jnp.dot(normed, diff, preferred_element_type=f32).astype(bf16)  15.2 us
    all_gather x1, waiting for transfers between devices, body(): gathered = lax.all_gather(hidden, 'mp', axis=1, tiled=True)  10.3 us
    psum x1, blocking collectives, body(): total_sq = lax.psum(jnp.sum(grads * grads), 'mp')  6.45 us
  transfers between devices with their start and end apart: 3, of which 3 were waited for; matrix products, arithmetic and copies ran while one was open for 0% of the time, Pallas kernels for 7%

profile of v1, /device:TPU:0, one launch (start us, length us, event | category | flops | bytes accessed | tf_op | source)
XLA Modules:
  0.0 310.4 jit_solution(5639888564733459395)
XLA Ops:
  7.2 0.0 all-gather.3.cloned.1.call-start
  7.2 2.3 copy.8
  9.5 0.0 all-gather.3.cloned.1.call-update
  9.6 0.0 all-reduce.2.cloned.1.call-start
  9.6 6.4 %all-gather = bf16[8192]{0:T(1024)(128)(2,1)S(1)} all-gather(bf16[2048]{0:T(1024)(128)(2,1)} %param.6), channel_id=2, replica_groups=mesh['dp'=8,'mp'=4] {'mp'}, dimensions={0}, use_global_device_ids=true | all-gather | bytes 20480 | tf_op jit(solution)/shard_map/all_gather | solution.py:136
  16.0 20.6 %shard_map.68 = (bf16[8192,512]{1,0:T(8,128)(2,1)}, bf16[8192,512]{1,0:T(8,128)(2,1)}, bf16[8192,512]{1,0:T(8,128)(2,1)}, f32[64,512]{1,0:T(8,128)}) custom-call(bf16[8192,512]{1,0:T(8,128)(2,1)} %w_ref.3, f32[64,512]{1,0:T(8,128)} %up_ref.3, f32[64,512]{1,0:T(8,128)} %low_ref.3), custom_call_target="tpu_custom_call" | custom-call | flops 125829120 | bytes 33554432 | tf_op jit(solution)/shard_map/pallas_call | solution.py:82
  36.6 10.3 %all-gather.3.cloned.1.call-done = bf16[256,8192]{0,1:T(8,128)(2,1)} async-done(((bf16[256,2048]{0,1:T(8,128)(2,1)}), bf16[256,8192]{0,1:T(8,128)(2,1)}) %all-gather.3.cloned.1.call-update) | async-done | bytes 4194320 | tf_op jit(solution)/shard_map/all_gather | solution.py:135
  46.9 0.0 copy-start
  46.9 3.5 %fusion = f32[256]{0:T(256)S(1)} fusion(bf16[256,8192]{0,1:T(8,128)(2,1)} %all-gather.3.cloned.1.call-done), kind=kLoop, calls=%fused_computation.2 | loop fusion | flops 6291200 | bytes 4195328 | tf_op jit(solution)/shard_map/reduce_sum | solution.py:138
  50.4 4.9 %fusion.5.nt_ref = bf16[8192,256]{1,0:T(8,128)(2,1)} fusion(f32[8192]{0:T(1024)S(1)} %mul.60, f32[256]{0:T(256)S(1)} %add_rsqrt_fusion, bf16[256,8192]{0,1:T(8,128)(2,1)} %all-gather.3.cloned.1.call-done), kind=kLoop, calls=%fused_computation.16 | loop fusion | flops 8388608 | bytes 8422400 | tf_op jit(solution)/shard_map/transpose | solution.py:140
  55.3 0.0 copy-done
  55.3 0.0 copy-done.3
  55.3 5.3 %convolution_convert_fusion.1.misfit_ref = bf16[256,512]{1,0:T(8,128)(2,1)} fusion(bf16[8192,512]{1,0:T(8,128)(2,1)S(1)} %copy-done.3, bf16[256,8192]{0,1:T(8,128)(2,1)S(1)} %copy-done, f32[8192]{0:T(1024)S(1)} %mul.60, f32[256]{0:T(256)S(1)} %add_rsqrt_fusion), kind=kOutput, calls=%fused_computation.6 | convolution fusion | flops 2156003328 | bytes 12878848 | tf_op jit(solution)/shard_map/dot_general | solution.py:148
  60.5 12.5 %shard_map.69 = f32[2,64,512]{2,1,0:T(8,128)} custom-call(bf16[8192,256]{1,0:T(8,128)(2,1)} %fusion.5.nt_ref, bf16[256,512]{1,0:T(8,128)(2,1)} %convolution_convert_fusion.1.misfit_ref, bf16[8192,512]{1,0:T(8,128)(2,1)} %get-tuple-element.11.h1_ref, bf16[8192,512]{1,0:T(8,128)(2,1)} %get-tuple-element.12.h2_ref, f32[64,512]{1,0:T(8,128)} %up_ref.3, ...), custom_call_target="tpu_custom_call" | custom-call | flops 2147483648 | bytes 20971520 | tf_op jit(solution)/shard_map/pallas_call | solution.py:117
  73.0 0.0 all-reduce.2.cloned.1.call-update
  73.1 0.0 reduce-scatter.2.cloned.1.call-start
  73.1 71.1 %all-reduce.2.cloned.1.call-done = f32[2,64,512]{2,1,0:T(8,128)} async-done(((f32[2,64,512]{2,1,0:T(8,128)}), f32[2,64,512]{2,1,0:T(8,128)}) %all-reduce.2.cloned.1.call-update) | async-done | bytes 262160 | tf_op jit(solution)/shard_map/psum | solution.py:151
  144.2 1.6 multiply_reduce_fusion
  145.8 6.4 %psum.22 = f32[]{:T(128)} all-reduce(f32[]{:T(128)} %multiply_reduce_fusion), channel_id=1, replica_groups=mesh['dp'=8,'mp'=4] {'mp'}, use_global_device_ids=true, to_apply=%region_3.0 | all-reduce | flops 1 | bytes 8 | tf_op jit(solution)/shard_map/psum | solution.py:152
  153.0 0.0 copy-done.1
  153.0 0.0 copy-done.2
  153.0 1.0 maximum_subtract_fusion
  154.0 0.7 slice_bitcast_fusion
  154.7 20.6 %shard_map.70 = (bf16[8192,512]{1,0:T(8,128)(2,1)}, bf16[8192,512]{1,0:T(8,128)(2,1)}, bf16[8192,512]{1,0:T(8,128)(2,1)}, f32[64,512]{1,0:T(8,128)}) custom-call(bf16[8192,512]{1,0:T(8,128)(2,1)} %w_ref.3, f32[64,512]{1,0:T(8,128)} %get-tuple-element.19.up_ref, f32[64,512]{1,0:T(8,128)} %get-tuple-element.18.low_ref), custom_call_target="tpu_custom_call" | custom-call | flops 125829120 | bytes 33554432 | tf_op jit(solution)/shard_map/pallas_call | solution.py:82
  175.3 9.9 %convolution_convert_fusion.misfit_ref = bf16[256,512]{1,0:T(8,128)(2,1)} fusion(bf16[8192,512]{1,0:T(8,128)(2,1)} %get-tuple-element.14, bf16[256,8192]{0,1:T(8,128)(2,1)} %all-gather.3.cloned.1.call-done, f32[8192]{0:T(1024)S(1)} %mul.60, f32[256]{0:T(256)S(1)} %add_rsqrt_fusion), kind=kOutput, calls=%fused_computation.5 | convolution fusion | flops 2156003328 | bytes 12878848 | tf_op jit(solution)/shard_map/dot_general | solution.py:148
  185.2 12.5 %shard_map.71 = f32[2,64,512]{2,1,0:T(8,128)} custom-call(bf16[8192,256]{1,0:T(8,128)(2,1)} %fusion.5.nt_ref, bf16[256,512]{1,0:T(8,128)(2,1)} %convolution_convert_fusion.misfit_ref, bf16[8192,512]{1,0:T(8,128)(2,1)} %get-tuple-element.15.h1_ref, bf16[8192,512]{1,0:T(8,128)(2,1)} %get-tuple-element.16.h2_ref, f32[64,512]{1,0:T(8,128)} %get-tuple-element.19.up_ref, ...), custom_call_target="tpu_custom_call" | custom-call | flops 2147483648 | bytes 20971520 | tf_op jit(solution)/shard_map/pallas_call | solution.py:117
  197.7 0.0 reduce-scatter.2.cloned.1.call-update
  197.7 62.3 %reduce-scatter.2.cloned.1.call-done = f32[2,8,512]{2,1,0:T(8,128)} async-done(((f32[2,64,512]{2,1,0:T(8,128)}), f32[2,8,512]{2,1,0:T(8,128)}) %reduce-scatter.2.cloned.1.call-update) | async-done | bytes 32784 | tf_op jit(solution)/shard_map/reduce_scatter | solution.py:154
  260.0 1.4 multiply_reduce_fusion.1
  261.4 40.3 %psum.23 = f32[]{:T(128)} all-reduce(f32[]{:T(128)} %multiply_reduce_fusion.1), channel_id=1, replica_groups=mesh['dp'=8,'mp'=4] {'dp','mp'}, use_global_device_ids=true, to_apply=%region_6.0 | all-reduce | flops 1 | bytes 8 | tf_op jit(solution)/shard_map/psum | solution.py:155
  302.4 0.8 divide_subtract_fusion
  303.2 0.6 slice_bitcast_fusion.2
  (5 shorter events, 0.0 us)
Async XLA Ops:
  7.2 39.7 %all-gather.3.cloned.1.call-start = ((), (), s32[]{:S(2)}) async-start(), calls=%async_computation.1 | async-start | bytes 5242880 | tf_op jit(solution)/shard_map/all_gather | solution.py:135
  9.6 134.7 %all-reduce.2.cloned.1.call-start = ((), (), s32[]{:S(2)}) async-start(), calls=%async_computation.2 | async-start | bytes 524288 | tf_op jit(solution)/shard_map/psum | solution.py:151
  46.9 8.4 %copy-start = (bf16[256,8192]{0,1:T(8,128)(2,1)S(1)}, bf16[256,8192]{0,1:T(8,128)(2,1)}, u32[]{:S(2)}) copy-start(bf16[256,8192]{0,1:T(8,128)(2,1)} %all-gather.3.cloned.1.call-done) | copy-start | bytes 12582916
  46.9 8.4 %copy-start.3 = (bf16[8192,512]{1,0:T(8,128)(2,1)S(1)}, bf16[8192,512]{1,0:T(8,128)(2,1)}, u32[]{:S(2)}) copy-start(bf16[8192,512]{1,0:T(8,128)(2,1)} %get-tuple-element.10) | copy-start | bytes 25165828
  60.5 92.5 %copy-start.1 = (f32[64,512]{1,0:T(8,128)S(1)}, f32[64,512]{1,0:T(8,128)}, u32[]{:S(2)}) copy-start(f32[64,512]{1,0:T(8,128)} %up_ref.3) | copy-start | bytes 393220
  60.5 92.5 %copy-start.2 = (f32[64,512]{1,0:T(8,128)S(1)}, f32[64,512]{1,0:T(8,128)}, u32[]{:S(2)}) copy-start(f32[64,512]{1,0:T(8,128)} %low_ref.3) | copy-start | bytes 393220
  73.1 187.0 %reduce-scatter.2.cloned.1.call-start = ((), (), s32[]{:S(2)}) async-start(), calls=%async_computation.3 | async-start | bytes 294912 | tf_op jit(solution)/shard_map/reduce_scatter | solution.py:154
Sparse Core Ops, SparseCore 0:
  9.7 37.1 all-gather.2
  73.2 70.9 all-reduce.1
  197.8 62.1 reduce-scatter.1

commit v2 on v1

--- a/solution.py
+++ b/solution.py
@@ -92,6 +92,112 @@
     )(weight, upper, lower)
 
 
+def gather_kernel(hidden_ref, gain_ref, w_ref, up_ref, low_ref, diff_ref, h1_ref, h2_ref, mag_ref, all_ref, gains_ref, par_ref, gain_send, gain_recv, own_send, own_recv, far_send, far_recv, near_send, near_recv, local_sem):
+    i, pieces = pl.program_id(0), pl.num_programs(0)
+    m = lax.axis_size("mp")
+    mine = lax.axis_index("mp")
+    chip, core = mine // 2, lax.rem(mine, 2)
+    chips = m // 2
+    sibling = chip * 2 + 1 - core
+    rows = hidden_ref.shape[0] // far_send.shape[1]
+
+    def own_copies():
+        copies = [
+            pltpu.make_async_copy(hidden_ref, all_ref.at[mine], local_sem.at[0]),
+            pltpu.make_async_copy(gain_ref, gains_ref.at[mine], local_sem.at[1]),
+        ]
+        for k in range(1, m):
+            copies.append(
+                pltpu.make_async_remote_copy(
+                    src_ref=gain_ref, dst_ref=gains_ref.at[mine], send_sem=gain_send.at[k],
+                    recv_sem=gain_recv.at[k], device_id={"mp": lax.rem(mine + k, m)},
+                )
+            )
+        copies.append(
+            pltpu.make_async_remote_copy(
+                src_ref=hidden_ref, dst_ref=all_ref.at[mine], send_sem=own_send,
+                recv_sem=own_recv, device_id={"mp": sibling},
+            )
+        )
+        return copies
+
+    def far_copy(k, p):
+        span = pl.ds(p * rows, rows)
+        return pltpu.make_async_remote_copy(
+            src_ref=hidden_ref.at[span], dst_ref=all_ref.at[mine, span], send_sem=far_send.at[k, p],
+            recv_sem=far_recv.at[k, p], device_id={"mp": lax.rem(chip + k, chips) * 2 + core},
+        )
+
+    def near_copy(k, p):
+        span = pl.ds(p * rows, rows)
+        source = lax.rem(chip + chips - k, chips) * 2 + core
+        return pltpu.make_async_remote_copy(
+            src_ref=all_ref.at[source, span], dst_ref=all_ref.at[source, span],
+            send_sem=near_send.at[k, p], recv_sem=near_recv.at[k, p], device_id={"mp": sibling},
+        )
+
+    @pl.when(i == 0)
+    def _():
+        barrier = pltpu.get_barrier_semaphore()
+        for k in range(1, m):
+            pl.semaphore_signal(barrier, inc=1, device_id={"mp": lax.rem(mine + k, m)})
+        pl.semaphore_wait(barrier, m - 1)
+        for p in range(far_send.shape[1]):
+            for k in range(1, chips):
+                far_copy(k, p).start()
+        for copy in own_copies():
+            copy.start()
+
+    forward_kernel(w_ref, up_ref, low_ref, diff_ref, h1_ref, h2_ref, mag_ref, par_ref)
+
+    for k in range(1, chips):
+        far_copy(k, i).wait_recv()
+        near_copy(k, i).start()
+
+    @pl.when(i == pieces - 1)
+    def _():
+        for copy in own_copies():
+            copy.wait()
+        for p in range(far_send.shape[1]):
+            for k in range(1, chips):
+                far_copy(k, p).wait_send()
+                near_copy(k, p).wait()
+
+
+def gather_forward(hidden, gain, weight, upper, lower):
+    rows, columns = weight.shape
+    groups = rows // GROUP
+    m = lax.axis_size("mp")
+    pieces = groups // CHUNK
+    gain = gain.reshape(-1, LANES)
+    big = pl.BlockSpec((CHUNK * GROUP, columns), lambda i: (i, 0))
+    small = pl.BlockSpec((CHUNK, columns), lambda i: (i, 0))
+    out = jax.ShapeDtypeStruct((rows, columns), bf16)
+    dma = pltpu.SemaphoreType.DMA
+    return pl.pallas_call(
+        gather_kernel,
+        grid=(pieces,),
+        in_specs=[
+            pl.BlockSpec(hidden.shape, lambda i: (0, 0)),
+            pl.BlockSpec(gain.shape, lambda i: (0, 0)),
+            big, small, small,
+        ],
+        out_specs=[big, big, big, small, pl.BlockSpec(memory_space=pl.ANY), pl.BlockSpec(memory_space=pl.ANY)],
+        out_shape=[
+            out, out, out, jax.ShapeDtypeStruct((groups, columns), f32),
+            jax.ShapeDtypeStruct((m,) + hidden.shape, bf16),
+            jax.ShapeDtypeStruct((m,) + gain.shape, bf16),
+        ],
+        scratch_shapes=[
+            pltpu.VMEM((5, CHUNK, columns), f32),
+            dma((m,)), dma((m,)), dma, dma,
+            dma((m // 2, pieces)), dma((m // 2, pieces)), dma((m // 2, pieces)), dma((m // 2, pieces)),
+            dma((2,)),
+        ],
+        compiler_params=pltpu.CompilerParams(collective_id=2, has_side_effects=True),
+    )(hidden, gain, weight, upper, lower)
+
+
 def backward_kernel(nt_ref, misfit_ref, h1_ref, h2_ref, up_ref, low_ref, mag_ref, grad_ref, sum_ref):
     chunk, columns = up_ref.shape
     for g in range(chunk):
@@ -131,32 +237,135 @@
     )(normed_t, misfit, h1, h2, upper, lower, magnitude)
 
 
+def update_kernel(last, count, grads_ref, params_ref, out_ref, parts, sums, squares, totals, send1, recv1, send2, recv2, send3, recv3):
+    n, m = lax.axis_size("dp"), lax.axis_size("mp")
+    me, mine = lax.axis_index("dp"), lax.axis_index("mp")
+
+    def peer(axis, size, index, k):
+        return {axis: lax.rem(index + k, size)}
+
+    barrier = pltpu.get_barrier_semaphore()
+    for k in range(1, n):
+        pl.semaphore_signal(barrier, inc=1, device_id=peer("dp", n, me, k))
+    for k in range(1, m):
+        pl.semaphore_signal(barrier, inc=1, device_id=peer("mp", m, mine, k))
+    pl.semaphore_wait(barrier, n + m - 2)
+
+    def exchange(axis, size, index, source, dest, send, recv):
+        copies = []
+        for k in range(1, size):
+            copies.append(
+                pltpu.make_async_remote_copy(
+                    src_ref=source(k), dst_ref=dest(k), send_sem=send.at[k], recv_sem=recv.at[k],
+                    device_id=peer(axis, size, index, k),
+                )
+            )
+            copies[-1].start()
+        return copies
+
+    copies = exchange(
+        "dp", n, me, lambda k: grads_ref.at[lax.rem(me + k, n)], lambda k: parts.at[k], send1, recv1
+    )
+    total = grads_ref[me]
+    for k, copy in enumerate(copies, 1):
+        copy.wait_recv()
+        total = total + parts[k]
+    columns = total.shape[1]
+    lanes = jnp.sum((total * total).reshape(-1, columns // LANES, LANES), axis=(0, 1))[None]
+    mine_sq = jnp.broadcast_to(lanes, (8, LANES))
+    if last:
+        squares[0] = mine_sq
+        gathers = exchange("dp", n, me, lambda k: squares.at[0], lambda k: squares.at[k], send2, recv2)
+    else:
+        sums[0] = total
+        gathers = exchange("dp", n, me, lambda k: sums.at[0], lambda k: sums.at[k], send2, recv2)
+    square = mine_sq
+    for k, copy in enumerate(gathers, 1):
+        copy.wait_recv()
+        if last:
+            square = square + squares[k]
+        else:
+            part = sums[k] * sums[k]
+            square = square + jnp.broadcast_to(
+                jnp.sum(part.reshape(-1, columns // LANES, LANES), axis=(0, 1))[None], (8, LANES)
+            )
+    totals[0] = square
+    finals = exchange("mp", m, mine, lambda k: totals.at[0], lambda k: totals.at[k], send3, recv3)
+    for k, copy in enumerate(finals, 1):
+        copy.wait_recv()
+        square = square + totals[k]
+    total_sq = jnp.sum(square[0:1], axis=1, keepdims=True)
+    scale = learn_rate / jnp.sqrt(total_sq / count + grad_eps)
+    if last:
+        out_ref[...] = params_ref[me] - scale * total
+    else:
+        out_ref[me] = params_ref[me] - scale * total
+        for k in range(1, n):
+            owner = lax.rem(me + n - k, n)
+            out_ref[owner] = params_ref[owner] - scale * sums[k]
+    for copy in copies + gathers + finals:
+        copy.wait_send()
+
+
+def update(last, count, grads, params):
+    n, rows, columns = grads.shape
+    m = lax.axis_size("mp")
+    whole = pl.BlockSpec(memory_space=pltpu.VMEM)
+    dma = pltpu.SemaphoreType.DMA
+    return pl.pallas_call(
+        functools.partial(update_kernel, last, count),
+        in_specs=[whole, whole],
+        out_specs=whole,
+        out_shape=jax.ShapeDtypeStruct((rows, columns) if last else (n, rows, columns), f32),
+        scratch_shapes=[
+            pltpu.VMEM((n, rows, columns), f32),
+            pltpu.VMEM((n, rows, columns), f32),
+            pltpu.VMEM((n, 8, LANES), f32),
+            pltpu.VMEM((m, 8, LANES), f32),
+            dma((n,)), dma((n,)), dma((n,)), dma((n,)), dma((m,)), dma((m,)),
+        ],
+        compiler_params=pltpu.CompilerParams(collective_id=1 if last else 0, has_side_effects=True),
+    )(grads, params)
+
+
+def pack(arrays, share):
+    _, groups, columns = arrays.shape
+    split = arrays.reshape(2, groups // share, share, columns)
+    return split.transpose(1, 0, 2, 3).reshape(groups // share, 2 * share, columns)
+
+
+def unpack(packed, share):
+    parts, _, columns = packed.shape
+    split = packed.reshape(parts, 2, share, columns).transpose(1, 0, 2, 3)
+    return split.reshape(2, parts * share, columns)
+
+
 def body(hidden, norm_gain, kv_weight, clip_upper, clip_lower):
-    gathered = lax.all_gather(hidden, "mp", axis=1, tiled=True)
-    gathered_gain = lax.all_gather(norm_gain[None, :], "mp", axis=1, tiled=True)
-    hidden_f = gathered.astype(f32)
-    mean_sq = jnp.mean(hidden_f * hidden_f, axis=1, keepdims=True)
-    normed = (hidden_f * lax.rsqrt(mean_sq + norm_eps) * gathered_gain[0].astype(f32)).astype(bf16)
-    normed_t = normed.T
+    *first, blocks, gains = gather_forward(hidden, norm_gain, kv_weight, clip_upper, clip_lower)
+    hidden_f = blocks.astype(f32)
+    m, tokens, features = blocks.shape
+    mean_sq = jnp.sum(hidden_f * hidden_f, axis=(0, 2), keepdims=True) / (m * features)
+    scaled = hidden_f * lax.rsqrt(mean_sq + norm_eps) * gains.reshape(m, 1, features).astype(f32)
+    normed_t = scaled.astype(bf16).transpose(0, 2, 1).reshape(m * features, tokens)
     groups = clip_upper.shape[0]
     param_count = 2 * groups * clip_upper.shape[1] * lax.axis_size("mp")
-    share_rows = groups // lax.axis_size("dp")
-    first_row = lax.axis_index("dp") * share_rows
-    params = jnp.stack([clip_upper, clip_lower])
+    share = groups // lax.axis_size("dp")
+    packed = pack(jnp.stack([clip_upper, clip_lower]), share)
+    upper, lower = clip_upper, clip_lower
     for iteration in range(STEPS):
-        diff, h1, h2, magnitude = forward(kv_weight, params[0], params[1])
-        misfit = jnp.dot(normed, diff, preferred_element_type=f32).astype(bf16)
-        grads = backward(normed_t, misfit, h1, h2, params[0], params[1], magnitude)
-        if iteration + 1 < STEPS:
-            grads = lax.psum(grads, "dp")
-            total_sq = lax.psum(jnp.sum(grads * grads), "mp")
+        if iteration == 0:
+            diff, h1, h2, magnitude = first
         else:
-            grads = lax.psum_scatter(grads, "dp", scatter_dimension=1, tiled=True)
-            total_sq = lax.psum(jnp.sum(grads * grads), ("dp", "mp"))
-            params = lax.dynamic_slice_in_dim(params, first_row, share_rows, 1)
-        grad_rms = jnp.sqrt(total_sq / param_count + grad_eps)
-        params = params - learn_rate * grads / grad_rms
-    return (params[0], params[1])
+            diff, h1, h2, magnitude = forward(kv_weight, upper, lower)
+        misfit = lax.dot_general(
+            normed_t, diff, (((0,), (0,)), ((), ())), preferred_element_type=f32
+        ).astype(bf16)
+        grads = pack(backward(normed_t, misfit, h1, h2, upper, lower, magnitude), share)
+        last = iteration + 1 == STEPS
+        packed = update(last, param_count, grads, packed)
+        if not last:
+            upper, lower = unpack(packed, share)
+    return (packed[:share], packed[share:])
 
 
 def solution(mesh):

time: 311 us -> 161 us (0.52)
  waiting for transfers between devices: 144 us -> 0 us
  Pallas kernels: 66.2 us -> 121 us
  blocking collectives: 53.2 us -> 0 us
  between operations: 15.2 us -> 0.67 us
  local copies, waits for them, and re-layouts: 3.66 us -> 11 us
    pallas_call x0 -> x3, Pallas kernels: none -> 75.9 us  [the longest x2 43.5 us: update(): pl.pallas_call(functools.partial(update_kernel, last, count), in_specs=[w...]
    psum x1 -> x0, waiting for transfers between devices: 71.1 us -> none  [body(): grads = lax.psum(grads, 'dp')]
    reduce_scatter x1 -> x0, waiting for transfers between devices: 62.3 us -> none  [body(): grads = lax.psum_scatter(grads, 'dp', scatter_dimension=1, tiled=True)]
    psum x2 -> x0, blocking collectives: 46.8 us -> none  [the longest x1 40.3 us: body(): total_sq = lax.psum(jnp.sum(grads * grads), ('dp', 'mp'))]
    pallas_call x2 -> x1, Pallas kernels: 41.2 us -> 20.6 us  [forward(): pl.pallas_call(forward_kernel, grid=(groups // CHUNK,), in_specs=[big, sm...]
    all_gather x1 -> x0, waiting for transfers between devices: 10.3 us -> none  [body(): gathered = lax.all_gather(hidden, 'mp', axis=1, tiled=True)]
    transpose x0 -> x2, local copies, waits for them, and re-layouts: none -> 7.21 us  [the longest x1 6.24 us: body(): scaled.astype(bf16).transpose(0, 2, 1).reshape(m * features, tokens)]
    all_gather x1 -> x0, blocking collectives: 6.41 us -> none  [body(): gathered_gain = lax.all_gather(norm_gain[None, :], 'mp', axis=1, tiled=True)]
  transfers between devices with their start and end apart: 3 -> 0, of which waited for: 3 -> 0; matrix products, arithmetic and copies ran while one was open for 0% -> 0% of each run, Pallas kernels for 7% -> 0%
where the time goes in v2:
time: 161 us; the launch traced here: 160 us
  Pallas kernels  121 us (75%)
  matrix products  15.4 us (10%)
  other arithmetic  11.4 us (7%)
  local copies, waits for them, and re-layouts  11 us (7%)
    pallas_call x2, Pallas kernels, update(): pl.pallas_call(functools.partial(update_kernel, last, count), in_specs=[w...  43.5 us
    pallas_call x1, Pallas kernels, gather_forward(): pl.pallas_call(gather_kernel, grid=(pieces,), in_specs=[pl.BlockSpec(hidd...  32.3 us
    pallas_call x2, Pallas kernels, backward(): pl.pallas_call(backward_kernel, grid=(groups // CHUNK,), in_specs=[pl.Blo...  25 us
    pallas_call x1, Pallas kernels, forward(): pl.pallas_call(forward_kernel, grid=(groups // CHUNK,), in_specs=[big, sm...  20.6 us
    dot_general x2, matrix products, body(): lax.dot_general(normed_t, diff, (((0,), (0,)), ((), ())), preferred_eleme...  15.4 us
    transpose x1, local copies, waits for them, and re-layouts, body(): scaled.astype(bf16).transpose(0, 2, 1).reshape(m * features, tokens)  6.24 us
    transpose x1, other arithmetic, body(): scaled.astype(bf16).transpose(0, 2, 1).reshape(m * features, tokens)  5.73 us

profile of v2, /device:TPU:0, one launch (start us, length us, event | category | flops | bytes accessed | tf_op | source)
XLA Modules:
  0.0 159.9 jit_solution(12305612806976221896)
XLA Ops:
  0.6 32.3 %shard_map.68 = (bf16[8192,512]{1,0:T(8,128)(2,1)}, bf16[8192,512]{1,0:T(8,128)(2,1)}, bf16[8192,512]{1,0:T(8,128)(2,1)}, f32[64,512]{1,0:T(8,128)}, bf16[4,256,...) custom-call(bf16[256,2048]{1,0:T(8,128)(2,1)} %hidden_ref.1, bf16[16,128]{1,0:T(8,128)(2,1)} %bitcast.53, ...), custom_call_target="tpu_custom_call" | custom-call | tf_op jit(solution)/shard_map/pallas_call | solution.py:177
  33.0 3.1 %fusion = f32[256]{0:T(256)S(1)} fusion(bf16[4,256,2048]{2,1,0:T(8,128)(2,1)} %get-tuple-element.12), kind=kLoop, calls=%fused_computation.2 | loop fusion | flops 6291200 | bytes 4195328 | tf_op jit(solution)/shard_map/reduce_sum | solution.py:347
  36.1 0.7 convert_bitcast_fusion
  36.8 5.7 %fusion.3 = bf16[4,2048,256]{1,2,0:T(8,128)(2,1)} fusion(bf16[4,256,2048]{2,1,0:T(8,128)(2,1)} %get-tuple-element.12, f32[4,2048]{1,0:T(4,128)S(1)} %bitcast.52, f32[256]{0:T(256)S(1)} %add_rsqrt_fusion), kind=kLoop, calls=%fused_computation.5 | loop fusion | flops 8388608 | bytes 8422400 | tf_op jit(solution)/shard_map/transpose | solution.py:349
  42.6 6.2 %copy.7 = bf16[4,2048,256]{2,1,0:T(8,128)(2,1)} copy(bf16[4,2048,256]{1,2,0:T(8,128)(2,1)} %fusion.3) | data formatting | bytes 8388608 | tf_op jit(solution)/shard_map/transpose | solution.py:349
  48.8 7.7 %convolution_convert_fusion.1.misfit_ref = bf16[256,512]{1,0:T(8,128)(2,1)} fusion(bf16[8192,256]{1,0:T(8,128)(2,1)} %bitcast.46, bf16[8192,512]{1,0:T(8,128)(2,1)} %get-tuple-element.14), kind=kOutput, calls=%fused_computation.7 | convolution fusion | flops 2147614720 | bytes 12845056 | tf_op jit(solution)/shard_map/dot_general | solution.py:360
  56.5 0.0 copy-start
  56.5 0.0 copy-start.1
  56.5 12.5 %shard_map.69 = f32[2,64,512]{2,1,0:T(8,128)} custom-call(bf16[8192,256]{1,0:T(8,128)(2,1)} %bitcast.47, bf16[256,512]{1,0:T(8,128)(2,1)} %convolution_convert_fusion.1.misfit_ref, bf16[8192,512]{1,0:T(8,128)(2,1)} %get-tuple-element.15.h1_ref, bf16[8192,512]{1,0:T(8,128)(2,1)} %get-tuple-element.16.h2_ref, f32[64,512]{1,0:T(8,128)} %up_ref.3, ...), custom_call_target="tpu_custom_call" | custom-call | flops 2147483648 | bytes 20971520 | tf_op jit(solution)/shard_map/pallas_call | solution.py:223
  69.0 0.0 copy-done
  69.0 0.0 copy-done.1
  69.0 1.8 %maximum_bitcast_fusion = (f32[8,16,512]{2,1,0:T(8,128)}, f32[8,16,512]{2,1,0:T(8,128)}) fusion(f32[1,8,8,512]{3,2,0,1:T(8,128)S(1)} %bitcast.51, f32[1,8,8,512]{3,2,0,1:T(8,128)S(1)} %bitcast.50, f32[2,64,512]{2,1,0:T(8,128)} %shard_map.69), kind=kLoop, calls=%fused_computation.8 | loop fusion | flops 65536 | bytes 1048576 | tf_op jit(solution)/shard_map/reshape | solution.py:334
  70.8 22.8 %shard_map.70.params_ref = f32[8,16,512]{2,1,0:T(8,128)} custom-call(f32[8,16,512]{2,1,0:T(8,128)} %get-tuple-element.27.grads_ref, f32[8,16,512]{2,1,0:T(8,128)} %get-tuple-element.26.params_ref), custom_call_target="tpu_custom_call" | custom-call | tf_op jit(solution)/shard_map/pallas_call | solution.py:315
  93.7 1.0 copy_bitcast_fusion.1
  94.7 0.7 slice_bitcast_fusion
  95.4 20.6 %shard_map.71 = (bf16[8192,512]{1,0:T(8,128)(2,1)}, bf16[8192,512]{1,0:T(8,128)(2,1)}, bf16[8192,512]{1,0:T(8,128)(2,1)}, f32[64,512]{1,0:T(8,128)}) custom-call(bf16[8192,512]{1,0:T(8,128)(2,1)} %w_ref.3, f32[64,512]{1,0:T(8,128)} %get-tuple-element.23.up_ref, f32[64,512]{1,0:T(8,128)} %get-tuple-element.22.low_ref), custom_call_target="tpu_custom_call" | custom-call | flops 125829120 | bytes 33554432 | tf_op jit(solution)/shard_map/pallas_call | solution.py:82
  116.0 7.7 %convolution_convert_fusion.misfit_ref = bf16[256,512]{1,0:T(8,128)(2,1)} fusion(bf16[8192,256]{1,0:T(8,128)(2,1)} %bitcast.48, bf16[8192,512]{1,0:T(8,128)(2,1)} %get-tuple-element.18), kind=kOutput, calls=%fused_computation.6 | convolution fusion | flops 2147614720 | bytes 12845056 | tf_op jit(solution)/shard_map/dot_general | solution.py:360
  123.7 12.5 %shard_map.72 = f32[2,64,512]{2,1,0:T(8,128)} custom-call(bf16[8192,256]{1,0:T(8,128)(2,1)} %bitcast.49, bf16[256,512]{1,0:T(8,128)(2,1)} %convolution_convert_fusion.misfit_ref, bf16[8192,512]{1,0:T(8,128)(2,1)} %get-tuple-element.19.h1_ref, bf16[8192,512]{1,0:T(8,128)(2,1)} %get-tuple-element.20.h2_ref, f32[64,512]{1,0:T(8,128)} %get-tuple-element.23.up_ref, ...), custom_call_target="tpu_custom_call" | custom-call | flops 2147483648 | bytes 20971520 | tf_op jit(solution)/shard_map/pallas_call | solution.py:223
  136.2 1.7 %copy_bitcast_fusion.grads_ref = f32[8,16,512]{2,1,0:T(8,128)} fusion(f32[2,64,512]{2,1,0:T(8,128)} %shard_map.72), kind=kLoop, calls=%fused_computation.9 | loop fusion | bytes 524288 | tf_op jit(solution)/shard_map/reshape | solution.py:334
  137.9 20.7 %shard_map.73 = f32[16,512]{1,0:T(8,128)} custom-call(f32[8,16,512]{2,1,0:T(8,128)} %copy_bitcast_fusion.grads_ref, f32[8,16,512]{2,1,0:T(8,128)} %shard_map.70.params_ref), custom_call_target="tpu_custom_call" | custom-call | tf_op jit(solution)/shard_map/pallas_call | solution.py:315
  158.6 1.3 fusion.4
  (2 shorter events, 0.0 us)
Async XLA Ops:
  56.5 12.5 %copy-start = (f32[64,512]{1,0:T(8,128)S(1)}, f32[64,512]{1,0:T(8,128)}, u32[]{:S(2)}) copy-start(f32[64,512]{1,0:T(8,128)} %up_ref.3) | copy-start | bytes 393220
  56.5 12.5 %copy-start.1 = (f32[64,512]{1,0:T(8,128)S(1)}, f32[64,512]{1,0:T(8,128)}, u32[]{:S(2)}) copy-start(f32[64,512]{1,0:T(8,128)} %low_ref.3) | copy-start | bytes 393220

commit v3 on v2

--- a/solution.py
+++ b/solution.py
@@ -101,9 +101,14 @@
     sibling = chip * 2 + 1 - core
     rows = hidden_ref.shape[0] // far_send.shape[1]
 
+    features = hidden_ref.shape[1]
+
+    def place(source):
+        return pl.ds(pl.multiple_of(source * features, LANES), features)
+
     def own_copies():
         copies = [
-            pltpu.make_async_copy(hidden_ref, all_ref.at[mine], local_sem.at[0]),
+            pltpu.make_async_copy(hidden_ref, all_ref.at[:, place(mine)], local_sem.at[0]),
             pltpu.make_async_copy(gain_ref, gains_ref.at[mine], local_sem.at[1]),
         ]
         for k in range(1, m):
@@ -115,7 +120,7 @@
             )
         copies.append(
             pltpu.make_async_remote_copy(
-                src_ref=hidden_ref, dst_ref=all_ref.at[mine], send_sem=own_send,
+                src_ref=hidden_ref, dst_ref=all_ref.at[:, place(mine)], send_sem=own_send,
                 recv_sem=own_recv, device_id={"mp": sibling},
             )
         )
@@ -124,7 +129,7 @@
     def far_copy(k, p):
         span = pl.ds(p * rows, rows)
         return pltpu.make_async_remote_copy(
-            src_ref=hidden_ref.at[span], dst_ref=all_ref.at[mine, span], send_sem=far_send.at[k, p],
+            src_ref=hidden_ref.at[span], dst_ref=all_ref.at[span, place(mine)], send_sem=far_send.at[k, p],
             recv_sem=far_recv.at[k, p], device_id={"mp": lax.rem(chip + k, chips) * 2 + core},
         )
 
@@ -132,7 +137,7 @@
         span = pl.ds(p * rows, rows)
         source = lax.rem(chip + chips - k, chips) * 2 + core
         return pltpu.make_async_remote_copy(
-            src_ref=all_ref.at[source, span], dst_ref=all_ref.at[source, span],
+            src_ref=all_ref.at[span, place(source)], dst_ref=all_ref.at[span, place(source)],
             send_sem=near_send.at[k, p], recv_sem=near_recv.at[k, p], device_id={"mp": sibling},
         )
 
@@ -185,7 +190,7 @@
         out_specs=[big, big, big, small, pl.BlockSpec(memory_space=pl.ANY), pl.BlockSpec(memory_space=pl.ANY)],
         out_shape=[
             out, out, out, jax.ShapeDtypeStruct((groups, columns), f32),
-            jax.ShapeDtypeStruct((m,) + hidden.shape, bf16),
+            jax.ShapeDtypeStruct((hidden.shape[0], m * hidden.shape[1]), bf16),
             jax.ShapeDtypeStruct((m,) + gain.shape, bf16),
         ],
         scratch_shapes=[
@@ -266,10 +271,10 @@
     copies = exchange(
         "dp", n, me, lambda k: grads_ref.at[lax.rem(me + k, n)], lambda k: parts.at[k], send1, recv1
     )
-    total = grads_ref[me]
+    total = grads_ref[me].astype(f32)
     for k, copy in enumerate(copies, 1):
         copy.wait_recv()
-        total = total + parts[k]
+        total = total + parts[k].astype(f32)
     columns = total.shape[1]
     lanes = jnp.sum((total * total).reshape(-1, columns // LANES, LANES), axis=(0, 1))[None]
     mine_sq = jnp.broadcast_to(lanes, (8, LANES))
@@ -318,7 +323,7 @@
         out_specs=whole,
         out_shape=jax.ShapeDtypeStruct((rows, columns) if last else (n, rows, columns), f32),
         scratch_shapes=[
-            pltpu.VMEM((n, rows, columns), f32),
+            pltpu.VMEM((n, rows, columns), bf16),
             pltpu.VMEM((n, rows, columns), f32),
             pltpu.VMEM((n, 8, LANES), f32),
             pltpu.VMEM((m, 8, LANES), f32),
@@ -343,10 +348,9 @@
 def body(hidden, norm_gain, kv_weight, clip_upper, clip_lower):
     *first, blocks, gains = gather_forward(hidden, norm_gain, kv_weight, clip_upper, clip_lower)
     hidden_f = blocks.astype(f32)
-    m, tokens, features = blocks.shape
-    mean_sq = jnp.sum(hidden_f * hidden_f, axis=(0, 2), keepdims=True) / (m * features)
-    scaled = hidden_f * lax.rsqrt(mean_sq + norm_eps) * gains.reshape(m, 1, features).astype(f32)
-    normed_t = scaled.astype(bf16).transpose(0, 2, 1).reshape(m * features, tokens)
+    mean_sq = jnp.mean(hidden_f * hidden_f, axis=1, keepdims=True)
+    normed = (hidden_f * lax.rsqrt(mean_sq + norm_eps) * gains.reshape(1, -1).astype(f32)).astype(bf16)
+    normed_t = normed.T
     groups = clip_upper.shape[0]
     param_count = 2 * groups * clip_upper.shape[1] * lax.axis_size("mp")
     share = groups // lax.axis_size("dp")
@@ -357,10 +361,8 @@
             diff, h1, h2, magnitude = first
         else:
             diff, h1, h2, magnitude = forward(kv_weight, upper, lower)
-        misfit = lax.dot_general(
-            normed_t, diff, (((0,), (0,)), ((), ())), preferred_element_type=f32
-        ).astype(bf16)
-        grads = pack(backward(normed_t, misfit, h1, h2, upper, lower, magnitude), share)
+        misfit = jnp.dot(normed, diff, preferred_element_type=f32).astype(bf16)
+        grads = pack(backward(normed_t, misfit, h1, h2, upper, lower, magnitude), share).astype(bf16)
         last = iteration + 1 == STEPS
         packed = update(last, param_count, grads, packed)
         if not last:

time: 161 us -> 157 us (0.975)
  Pallas kernels: 121 us -> 116 us
  matrix products: 15.4 us -> 19.9 us
    pallas_call x0 -> x1, local copies, waits for them, and re-layouts: none -> 6.36 us  [gather_forward(): pl.pallas_call(gather_kernel, grid=(pieces,), in_specs=[pl.BlockSpec(hidd...]
    transpose x1 -> x0, local copies, waits for them, and re-layouts: 6.24 us -> none  [body(): scaled.astype(bf16).transpose(0, 2, 1).reshape(m * features, tokens)]
    pallas_call x2, Pallas kernels: 43.5 us -> 37.7 us  [update(): pl.pallas_call(functools.partial(update_kernel, last, count), in_specs=[w...]
    dot_general x2, matrix products: 15.4 us -> 19.9 us  [body(): misfit = jnp.dot(normed, diff, preferred_element_type=f32).astype(bf16)]
    convert_element_type x0 -> x3, other arithmetic: none -> 3.24 us  [the longest x2 3.23 us: body(): pack(backward(normed_t, misfit, h1, h2, upper, lower, magnitude), share)]
    transpose x1, other arithmetic: 5.73 us -> 2.56 us  [body(): normed_t = normed.T]
    reshape x1 -> x0, local copies, waits for them, and re-layouts: 1.67 us -> none  [pack(): split.transpose(1, 0, 2, 3).reshape(groups // share, 2 * share, columns)]
where the time goes in v3:
time: 157 us; the launch traced here: 156 us
  Pallas kernels  116 us (74%)
  matrix products  19.9 us (13%)
  other arithmetic  10.8 us (7%)
  local copies, waits for them, and re-layouts  9.4 us (6%)
    pallas_call x2, Pallas kernels, update(): pl.pallas_call(functools.partial(update_kernel, last, count), in_specs=[w...  37.7 us
    pallas_call x1, Pallas kernels, gather_forward(): pl.pallas_call(gather_kernel, grid=(pieces,), in_specs=[pl.BlockSpec(hidd...  32.3 us
    pallas_call x2, Pallas kernels, backward(): pl.pallas_call(backward_kernel, grid=(groups // CHUNK,), in_specs=[pl.Blo...  25 us
    pallas_call x1, Pallas kernels, forward(): pl.pallas_call(forward_kernel, grid=(groups // CHUNK,), in_specs=[big, sm...  20.6 us
    dot_general x2, matrix products, body(): misfit = jnp.dot(normed, diff, preferred_element_type=f32).astype(bf16)  19.9 us
    pallas_call x1, local copies, waits for them, and re-layouts, gather_forward(): pl.pallas_call(gather_kernel, grid=(pieces,), in_specs=[pl.BlockSpec(hidd...  6.36 us
    reduce_sum x1, other arithmetic, body(): mean_sq = jnp.mean(hidden_f * hidden_f, axis=1, keepdims=True)  3.3 us
    convert_element_type x2, other arithmetic, body(): pack(backward(normed_t, misfit, h1, h2, upper, lower, magnitude), share)  3.23 us

profile of v3, /device:TPU:0, one launch (start us, length us, event | category | flops | bytes accessed | tf_op | source)
XLA Modules:
  0.0 156.4 jit_solution(17388459766698989035)
XLA Ops:
  0.6 1.7 %maximum_bitcast_fusion.params_ref = f32[8,16,512]{2,1,0:T(8,128)} fusion(f32[1,8,8,512]{3,2,0,1:T(8,128)} %bitcast.41, f32[1,8,8,512]{3,2,0,1:T(8,128)} %bitcast.40), kind=kLoop, calls=%fused_computation.7 | loop fusion | flops 65536 | bytes 524288 | tf_op jit(solution)/shard_map/reshape | solution.py:339
  2.3 32.3 %shard_map.68 = (bf16[8192,512]{1,0:T(8,128)(2,1)}, bf16[8192,512]{1,0:T(8,128)(2,1)}, bf16[8192,512]{1,0:T(8,128)(2,1)}, f32[64,512]{1,0:T(8,128)}, bf16[256,81...) custom-call(bf16[256,2048]{1,0:T(8,128)(2,1)} %hidden_ref.1, bf16[16,128]{1,0:T(8,128)(2,1)} %bitcast.43, ...), custom_call_target="tpu_custom_call" | custom-call | tf_op jit(solution)/shard_map/pallas_call | solution.py:182
  34.6 0.0 copy-start.1
  34.6 6.4 %copy.7 = bf16[256,8192]{0,1:T(8,128)(2,1)} copy(bf16[256,8192]{1,0:T(8,128)(2,1)} %get-tuple-element.12) | data formatting | bytes 8388608 | tf_op jit(solution)/shard_map/pallas_call | solution.py:182
  41.0 3.3 %fusion = f32[256]{0:T(256)S(1)} fusion(bf16[256,8192]{0,1:T(8,128)(2,1)} %copy.7), kind=kLoop, calls=%fused_computation.2 | loop fusion | flops 6291200 | bytes 4195328 | tf_op jit(solution)/shard_map/reduce_sum | solution.py:351
  44.3 0.0 copy-done.1
  44.3 0.0 copy-start
  44.3 10.0 %convolution_convert_fusion.1.misfit_ref = bf16[256,512]{1,0:T(8,128)(2,1)} fusion(bf16[8192,512]{1,0:T(8,128)(2,1)} %get-tuple-element.14, bf16[256,8192]{0,1:T(8,128)(2,1)} %copy.7, f32[8192]{0:T(1024)S(1)} %convert.1, f32[256]{0:T(256)S(1)} %add_rsqrt_fusion), kind=kOutput, calls=%fused_computation.6 | convolution fusion | flops 2156003328 | bytes 12878848 | tf_op jit(solution)/shard_map/dot_general | solution.py:364
  54.4 0.0 copy-done
  54.4 2.6 %fusion.5.nt_ref = bf16[8192,256]{1,0:T(8,128)(2,1)} fusion(f32[8192]{0:T(1024)S(1)} %convert.1, f32[256]{0:T(256)S(1)} %add_rsqrt_fusion, bf16[256,8192]{0,1:T(8,128)(2,1)S(1)} %copy-done), kind=kLoop, calls=%fused_computation.16 | loop fusion | flops 8388608 | bytes 8422400 | tf_op jit(solution)/shard_map/transpose | solution.py:353
  56.9 12.5 %shard_map.69 = f32[2,64,512]{2,1,0:T(8,128)} custom-call(bf16[8192,256]{1,0:T(8,128)(2,1)} %fusion.5.nt_ref, bf16[256,512]{1,0:T(8,128)(2,1)} %convolution_convert_fusion.1.misfit_ref, bf16[8192,512]{1,0:T(8,128)(2,1)} %get-tuple-element.15.h1_ref, bf16[8192,512]{1,0:T(8,128)(2,1)} %get-tuple-element.16.h2_ref, f32[64,512]{1,0:T(8,128)} %up_ref.3, ...), custom_call_target="tpu_custom_call" | custom-call | flops 2147483648 | bytes 20971520 | tf_op jit(solution)/shard_map/pallas_call | solution.py:228
  69.4 1.6 %copy_bitcast_fusion.2.grads_ref = bf16[8,16,512]{2,1,0:T(8,128)(2,1)} fusion(f32[2,64,512]{2,1,0:T(8,128)} %shard_map.69), kind=kLoop, calls=%fused_computation.12 | loop fusion | flops 65536 | bytes 393216 | tf_op jit(solution)/shard_map/convert_element_type | solution.py:365
  71.0 20.2 %shard_map.70.params_ref = f32[8,16,512]{2,1,0:T(8,128)} custom-call(bf16[8,16,512]{2,1,0:T(8,128)(2,1)} %copy_bitcast_fusion.2.grads_ref, f32[8,16,512]{2,1,0:T(8,128)} %maximum_bitcast_fusion.params_ref), custom_call_target="tpu_custom_call" | custom-call | tf_op jit(solution)/shard_map/pallas_call | solution.py:320
  91.3 1.0 copy_bitcast_fusion
  92.2 0.7 slice_bitcast_fusion
  93.0 20.6 %shard_map.71 = (bf16[8192,512]{1,0:T(8,128)(2,1)}, bf16[8192,512]{1,0:T(8,128)(2,1)}, bf16[8192,512]{1,0:T(8,128)(2,1)}, f32[64,512]{1,0:T(8,128)}) custom-call(bf16[8192,512]{1,0:T(8,128)(2,1)} %w_ref.3, f32[64,512]{1,0:T(8,128)} %get-tuple-element.23.up_ref, f32[64,512]{1,0:T(8,128)} %get-tuple-element.22.low_ref), custom_call_target="tpu_custom_call" | custom-call | flops 125829120 | bytes 33554432 | tf_op jit(solution)/shard_map/pallas_call | solution.py:82
  113.6 9.9 %convolution_convert_fusion.misfit_ref = bf16[256,512]{1,0:T(8,128)(2,1)} fusion(bf16[8192,512]{1,0:T(8,128)(2,1)} %get-tuple-element.18, bf16[256,8192]{0,1:T(8,128)(2,1)} %copy.7, f32[8192]{0:T(1024)S(1)} %convert.1, f32[256]{0:T(256)S(1)} %add_rsqrt_fusion), kind=kOutput, calls=%fused_computation.5 | convolution fusion | flops 2156003328 | bytes 12878848 | tf_op jit(solution)/shard_map/dot_general | solution.py:364
  123.5 12.5 %shard_map.72 = f32[2,64,512]{2,1,0:T(8,128)} custom-call(bf16[8192,256]{1,0:T(8,128)(2,1)} %fusion.5.nt_ref, bf16[256,512]{1,0:T(8,128)(2,1)} %convolution_convert_fusion.misfit_ref, bf16[8192,512]{1,0:T(8,128)(2,1)} %get-tuple-element.19.h1_ref, bf16[8192,512]{1,0:T(8,128)(2,1)} %get-tuple-element.20.h2_ref, f32[64,512]{1,0:T(8,128)} %get-tuple-element.23.up_ref, ...), custom_call_target="tpu_custom_call" | custom-call | flops 2147483648 | bytes 20971520 | tf_op jit(solution)/shard_map/pallas_call | solution.py:228
  135.9 1.6 %copy_bitcast_fusion.1.grads_ref = bf16[8,16,512]{2,1,0:T(8,128)(2,1)} fusion(f32[2,64,512]{2,1,0:T(8,128)} %shard_map.72), kind=kLoop, calls=%fused_computation.11 | loop fusion | flops 65536 | bytes 393216 | tf_op jit(solution)/shard_map/convert_element_type | solution.py:365
  137.6 17.5 %shard_map.73 = f32[16,512]{1,0:T(8,128)} custom-call(bf16[8,16,512]{2,1,0:T(8,128)(2,1)} %copy_bitcast_fusion.1.grads_ref, f32[8,16,512]{2,1,0:T(8,128)} %shard_map.70.params_ref), custom_call_target="tpu_custom_call" | custom-call | tf_op jit(solution)/shard_map/pallas_call | solution.py:320
  155.0 1.3 fusion.6
  (2 shorter events, 0.0 us)
Async XLA Ops:
  34.6 9.7 %copy-start.1 = (bf16[4,16,128]{2,1,0:T(8,128)(2,1)S(1)}, bf16[4,16,128]{2,1,0:T(8,128)(2,1)}, u32[]{:S(2)}) copy-start(bf16[4,16,128]{2,1,0:T(8,128)(2,1)} %get-tuple-element.13) | copy-start | bytes 49156
  44.3 10.0 %copy-start = (bf16[256,8192]{0,1:T(8,128)(2,1)S(1)}, bf16[256,8192]{0,1:T(8,128)(2,1)}, u32[]{:S(2)}) copy-start(bf16[256,8192]{0,1:T(8,128)(2,1)} %copy.7) | copy-start | bytes 12582916
